TPU v7x, 128 devices: a whole 4x4x4 slice. The times are simulated.
128 devices in a mesh: ma: 64 (over x_hi, y, z, core), row: 2 (over x_lo).
Axes of the slice: x: 4 (x_hi: 2, x_lo: 2; x = x_hi * 2 + x_lo), y: 4, z: 4, core: 2. Of those that a mesh axis runs over, the one named last changes fastest.
Arguments:
- spectral: bfloat16 [384, 2, 384, 2, 769], P('ma', None, 'row'), may hold values from -0.011047363 to 0.011047363
- latitude_basis: bfloat16 [384, 769, 1152], P('ma'), may hold values from -0.21875 to 0.21875
- pair_orders: int32 [384], replicated, may hold values from 0 to 383, each once
Outputs:
- grid_values: bfloat16 [64, 2, 1152, 2304], P('row', None, 'ma')
Inputs may be any that keep to these rules, and one draw needn't show every extreme that they name: A permutation of 0 to 383; slot p holds the orders pair_orders[p] and 767 - pair_orders[p].
All inputs are finite; a program needn't handle non-finite values.
Results may differ from a plain program's by a relative error of at most 0.0066.
Values may be sent and summed in bfloat16 or wider, within the bound.
A program may use at most 128 MiB of HBM per device.

v0:
```python
import math

import jax
import jax.numpy as jnp
from jax import lax
from jax.sharding import PartitionSpec as P

NLON = 2304
LEV = 64


def cut_along(shard, dim, size):
    before, after = (shard.shape[:dim], shard.shape[dim + 1 :])
    return jnp.moveaxis(shard.reshape(*before, size, -1, *after), dim, 0)


def sum_at_owner(shard, axis, dim):
    tiles = cut_along(shard, dim, lax.axis_size(axis))
    arrived = lax.all_to_all(tiles, axis, split_axis=0, concat_axis=0, tiled=True)
    return arrived.sum(axis=0)


def radial_table(total_modes, levels):
    mode_index = lax.broadcasted_iota(jnp.int32, (total_modes, levels), 0)
    points = lax.broadcasted_iota(jnp.int32, (total_modes, levels), 1)
    period = 2 * (total_modes - 1)
    phase_steps = mode_index * points % period
    return jnp.cos(phase_steps.astype(jnp.float32) * (2.0 * math.pi / period)).astype(jnp.bfloat16)


def longitude_table(pair_orders, degrees, points):
    orders = jnp.stack([pair_orders, degrees - 1 - pair_orders], axis=1)
    weights = jnp.where(orders == 0, 1.0, 2.0).astype(jnp.float32)
    phase_index = orders[:, :, None] * lax.broadcasted_iota(jnp.int32, (1, 1, points), 2) % points
    angles = phase_index.astype(jnp.float32) * (2.0 * math.pi / points)
    real_part = weights[:, :, None] * jnp.cos(angles)
    imag_part = -weights[:, :, None] * jnp.sin(angles)
    stacked = jnp.stack([real_part, imag_part], axis=2)
    return stacked.reshape(-1, points).astype(jnp.bfloat16)


def order_selectors(local_orders, degrees, packed):
    packed_rows = lax.broadcasted_iota(jnp.int32, (local_orders.shape[0], packed), 1)
    below_split = packed_rows < (degrees - local_orders)[:, None]
    return jnp.stack([below_split, jnp.logical_not(below_split)], axis=1).astype(jnp.bfloat16)


def per_device(spectral, latitude_basis, pair_orders):
    pair_dev = spectral.shape[0]
    local_modes = spectral.shape[2]
    fields = spectral.shape[3]
    packed = spectral.shape[4]
    degrees = packed - 1
    row_count = lax.axis_size("row")
    total_modes = local_modes * row_count
    level_dev = LEV // row_count
    cheb_table = radial_table(total_modes, LEV)
    own_rows = lax.dynamic_slice_in_dim(
        cheb_table, lax.axis_index("row") * local_modes, local_modes, 0
    )
    scattered = sum_at_owner(
        jnp.einsum("pckfr,kl->lpcfr", spectral, own_rows, preferred_element_type=jnp.float32),
        "row",
        0,
    )
    summed = jnp.transpose(scattered, (1, 2, 0, 3, 4))
    levels = summed.astype(jnp.bfloat16)
    local_orders = lax.dynamic_slice_in_dim(
        pair_orders, lax.axis_index("ma") * pair_dev, pair_dev, 0
    )
    selectors = order_selectors(local_orders, degrees, packed)
    masked = levels[:, None] * selectors[:, :, None, None, None, :]
    lon_table = longitude_table(pair_orders, degrees, NLON)
    block_levels = masked.shape[3]
    fourier = jnp.einsum(
        "phclfr,prt->phclft", masked, latitude_basis, preferred_element_type=jnp.float32
    ).astype(jnp.bfloat16)
    fourier = fourier.reshape(pair_dev * 4, block_levels * fields, fourier.shape[-1])
    synthesized = jnp.einsum(
        "oit,on->itn",
        lax.all_to_all(fourier, "ma", split_axis=2, concat_axis=0, tiled=True),
        lon_table,
        preferred_element_type=jnp.float32,
    ).astype(jnp.bfloat16)
    return synthesized.reshape(level_dev, fields, synthesized.shape[1], synthesized.shape[2])


def solution(mesh):
    return jax.shard_map(
        per_device,
        mesh=mesh,
        in_specs=(P("ma", None, "row", None, None), P("ma", None, None), P()),
        out_specs=P("row", None, "ma", None),
        check_vma=False,
    )
```

profile of v0, /device:TPU:1, one launch (start us, length us, event | category | flops | bytes accessed | tf_op | source)
XLA Modules:
  0.0 249.0 jit_solution(5887593819390033266)
XLA Ops:
  0.0 0.1 fusion.15
  0.1 5.3 %fusion.2 = f32[64,6,2,2,769]{4,0,3,2,1:T(8,128)S(1)} fusion(bf16[6,2,192,2,769]{4,3,2,1,0:T(2,128)(2,1)} %param.3, s32[384,64]{0,1:T(8,128)S(1)} %multiply_remainder_fusion.1, s32[]{:T(128)S(6)} %select_n.42, pred[384,64]{0,1:T(32,128)(4,1)S(1)} %get-tuple-element.11, pred[384,64]{0,1:T(32,128)(4,1)S(1)} %get-tuple-element.12), kind=kOutput, calls=%fused_computation.3 | convolution fusion | flops 453648384 | bytes 11910148 | tf_op jit(solution)/shard_map/pckfr,kl->lpcfr/dot_general | solution.py:62
  5.4 2.9 %copy.33 = f32[2,32,6,2,2,769]{5,1,4,3,2,0:T(8,128)} copy(f32[2,32,6,2,2,769]{5,1,0,4,3,2:T(8,128)S(1)} %bitcast.31) | data formatting | bytes 9449472 | tf_op jit(solution)/shard_map/reshape | solution.py:14
  8.4 0.0 copy-start
  8.4 6.2 %all-to-all-start = ((f32[2,32,6,2,2,769]{5,1,4,3,2,0:T(8,128)}), f32[2,32,6,2,2,769]{5,1,4,3,2,0:T(8,128)}, u32[]{:S(2)}, u32[]{:S(2)}) async-start(f32[2,32,6,2,2,769]{5,1,4,3,2,0:T(8,128)} %copy.33), calls=%async_computation | async-start | bytes 11010048 | tf_op jit(solution)/shard_map/all_to_all | solution.py:19
  14.6 0.0 copy-done
  14.6 0.1 dynamic-slice_subtract_fusion
  14.7 0.1 iota_compare_fusion
  14.8 0.1 add_convert_fusion
  14.8 61.1 %all-to-all-done = f32[2,32,6,2,2,769]{5,1,4,3,2,0:T(8,128)} async-done(((f32[2,32,6,2,2,769]{5,1,4,3,2,0:T(8,128)}), f32[2,32,6,2,2,769]{5,1,4,3,2,0:T(8,128)}, u32[]{:S(2)}, u32[]{:S(2)}) %all-to-all-start) | async-done | bytes 4724768 | tf_op jit(solution)/shard_map/all_to_all | solution.py:19
  76.0 3.3 %reduce_sum.9 = bf16[32,6,2,2,769]{4,0,3,2,1:T(8,128)(2,1)S(1)} reduce(f32[2,32,6,2,2,769]{5,1,4,3,2,0:T(8,128)} %all-to-all-done, f32[]{:T(128)} %constant.24.clone.1), dimensions={0}, to_apply=%region_0.1 | reduce | flops 590592 | bytes 5905924 | tf_op jit(solution)/shard_map/reduce_sum | solution.py:20
  79.3 8.5 %fusion.9 = bf16[6,2,2,32,2,1152]{5,3,4,2,1,0:T(8,128)(2,1)S(1)} fusion(bf16[6,769,1152]{2,1,0:T(8,128)(2,1)} %param.4, bf16[6,2,769]{2,1,0:T(2,128)(2,1)S(1)} %add_convert_fusion, bf16[6,2,32,2,769]{4,2,3,1,0:T(8,128)(2,1)S(1)} %bitcast.32), kind=kOutput, calls=%fused_computation.15 | convolution fusion | flops 2724398592 | bytes 15369240 | tf_op jit(solution)/shard_map/phclfr,prt->phclft/dot_general | solution.py:75
  87.8 3.5 %copy.34 = bf16[6,2,2,32,2,1152]{5,4,3,2,1,0:T(2,128)(2,1)S(1)} copy(bf16[6,2,2,32,2,1152]{5,3,4,2,1,0:T(8,128)(2,1)S(1)} %fusion.9) | data formatting | bytes 7077888 | tf_op jit(solution)/shard_map/convert_element_type | solution.py:77
  91.3 3.4 %reshape.156 = bf16[24,64,1152]{2,1,0:T(8,128)(2,1)} reshape(bf16[6,2,2,32,2,1152]{5,4,3,2,1,0:T(2,128)(2,1)S(1)} %copy.34) | data formatting | bytes 7077888 | tf_op jit(solution)/shard_map/reshape | solution.py:78
  94.7 9.0 %copy.35 = bf16[24,64,1152]{1,0,2:T(8,128)(2,1)} copy(bf16[24,64,1152]{2,1,0:T(8,128)(2,1)} %reshape.156) | data formatting | bytes 7077888 | tf_op jit(solution)/shard_map/reshape | solution.py:78
  103.6 12.2 %reshape.162 = bf16[64,2,13824]{2,1,0:T(2,128)(2,1)} reshape(bf16[1152,24,64]{2,1,0:T(8,128)(2,1)} %bitcast.30) | data formatting | bytes 7077888
  115.8 12.9 %all-to-all-start.1 = ((bf16[64,2,13824]{2,1,0:T(2,128)(2,1)}), bf16[64,2,13824]{2,1,0:T(2,128)(2,1)}, u32[]{:S(2)}, u32[]{:S(2)}) async-start(bf16[64,2,13824]{2,1,0:T(2,128)(2,1)} %reshape.162), calls=%async_computation.1 | async-start | bytes 7077888 | tf_op jit(solution)/shard_map/all_to_all | solution.py:81
  128.8 31.0 %multiply_convert_fusion.1 = (bf16[384,2,1,2304]{3,0,2,1:T(8,128)(2,1)S(1)}, bf16[384,2,1,2304]{3,0,2,1:T(8,128)(2,1)S(1)}) fusion(s32[384,2]{0,1:T(2,128)S(1)} %pad_add_fusion, f32[384,2]{0,1:T(2,128)S(1)} %get-tuple-element.7, f32[384,2]{0,1:T(2,128)S(1)} %get-tuple-element.8), kind=kLoop, calls=%fused_computation.9 | loop fusion | flops 23003136 | bytes 7087104 | tf_op jit(solution)/shard_map/convert
  159.8 0.6 pad_maximum_fusion
  160.5 21.3 %copy.37 = bf16[384,2,2,2304]{3,2,1,0:T(2,128)(2,1)} copy(bf16[384,2,2,2304]{3,0,2,1:T(8,128)(2,1)S(1)} %pad_maximum_fusion) | data formatting | bytes 14155776 | tf_op jit(solution)/shard_map/stack | solution.py:38
  181.7 15.1 %reshape.160 = bf16[1536,2304,1]{1,0,2:T(8,128)(2,1)} reshape(bf16[384,2,2,2304]{3,2,1,0:T(2,128)(2,1)} %copy.37) | data formatting | bytes 14155776 | tf_op jit(solution)/shard_map/convert_element_type | solution.py:39
  196.9 0.0 all-to-all-done.1
  196.9 0.0 slice-start
  196.9 12.5 %reshape.163 = bf16[1152,24,64]{2,1,0:T(8,128)(2,1)} reshape(bf16[64,2,13824]{2,1,0:T(2,128)(2,1)} %all-to-all-done.1) | data formatting | bytes 7077888
  209.4 0.0 slice-start.1
  209.4 7.9 %copy.36 = bf16[64,24,64,18]{2,1,0,3:T(8,128)(2,1)} copy(bf16[64,24,64,18]{2,1,3,0:T(8,128)(2,1)} %bitcast.29) | data formatting | bytes 7077888 | tf_op jit(solution)/shard_map/all_to_all | solution.py:81
  217.3 0.0 slice-done
  217.3 0.0 slice-done.1
  217.3 14.5 %convolution_convert_fusion = bf16[64,18,2304]{2,0,1:T(8,128)(2,1)} fusion(bf16[1536,64,18]{1,0,2:T(8,128)(2,1)} %bitcast.28, bf16[1536,2304,1]{1,0,2:T(8,128)(2,1)S(1)} %bitcast.27), kind=kOutput, calls=%fused_computation.14 | convolution fusion | flops 8156381184 | bytes 15925248 | tf_op jit(solution)/shard_map/oit,on->itn/dot_general | solution.py:79
  231.8 11.2 %reshape.157 = bf16[32,2,18,2304]{3,1,0,2:T(2,128)(2,1)} reshape(bf16[64,18,2304]{2,0,1:T(8,128)(2,1)} %convolution_convert_fusion) | data formatting | bytes 10616832 | tf_op jit(solution)/shard_map/reshape | solution.py:85
  242.9 6.1 %copy.39 = bf16[32,2,18,2304]{3,1,2,0:T(2,128)(2,1)} copy(bf16[32,2,18,2304]{3,1,0,2:T(2,128)(2,1)} %reshape.157) | data formatting | bytes 10616832 | tf_op jit(solution)/shard_map/reshape | solution.py:85
  (7 shorter events, 0.1 us)
Async XLA Ops:
  8.4 6.2 %copy-start = (s32[384]{0:T(512)S(1)}, s32[384]{0:T(512)}, u32[]{:S(2)}) copy-start(s32[384]{0:T(512)} %param.5) | copy-start | bytes 4612
  8.4 67.6 %all-to-all-start = ((f32[2,32,6,2,2,769]{5,1,4,3,2,0:T(8,128)}), f32[2,32,6,2,2,769]{5,1,4,3,2,0:T(8,128)}, u32[]{:S(2)}, u32[]{:S(2)}) async-start(f32[2,32,6,2,2,769]{5,1,4,3,2,0:T(8,128)} %copy.33), calls=%async_computation | async-start | bytes 11010048 | tf_op jit(solution)/shard_map/all_to_all | solution.py:19
  115.8 81.1 %all-to-all-start.1 = ((bf16[64,2,13824]{2,1,0:T(2,128)(2,1)}), bf16[64,2,13824]{2,1,0:T(2,128)(2,1)}, u32[]{:S(2)}, u32[]{:S(2)}) async-start(bf16[64,2,13824]{2,1,0:T(2,128)(2,1)} %reshape.162), calls=%async_computation.1 | async-start | bytes 7077888 | tf_op jit(solution)/shard_map/all_to_all | solution.py:81
  196.9 20.4 %slice-start = ((s8[7077888]{0:T(1024)(128)(4,1)}), s8[2883584]{0:T(1024)(128)(4,1)S(1)}, s32[]{:S(2)}) async-start(s8[7077888]{0:T(1024)(128)(4,1)} %bitcast.26), calls=%async_computation.2 | async-start | bytes 5767168
  209.4 7.9 %slice-start.1 = ((s8[7077888]{0:T(1024)(128)(4,1)}), s8[4194304]{0:T(1024)(128)(4,1)S(1)}, s32[]{:S(2)}) async-start(s8[7077888]{0:T(1024)(128)(4,1)} %bitcast.26), calls=%async_computation.3 | async-start | bytes 8388608
where the time goes:
time: 251 us; the launch traced here: 249 us
  local copies, waits for them, and re-layouts  105 us (42%)
  waiting for transfers between devices  61.1 us (24%)
  other arithmetic  35.3 us (14%)
  matrix products  28.3 us (11%)
  starting transfers between devices  19.1 us (8%)
    all_to_all x1, waiting for transfers between devices, sum_at_owner(): lax.all_to_all(tiles, axis, split_axis=0, concat_axis=0, tiled=True)  61.1 us
    another operation x1, other arithmetic  31 us
    unnamed x8, local copies, waits for them, and re-layouts  24.7 us
    another operation x1, local copies, waits for them, and re-layouts, longitude_table(): stacked = jnp.stack([real_part, imag_part], axis=2)  21.3 us
    reshape x2, local copies, waits for them, and re-layouts, per_device(): synthesized.reshape(level_dev, fields, synthesized.shape[1], synthesized....  17.3 us
    convert_element_type x1, local copies, waits for them, and re-layouts, longitude_table(): return stacked.reshape(-1, points).astype(jnp.bfloat16)  15.1 us
    dot_general x1, matrix products, per_device(): jnp.einsum('oit,on->itn', lax.all_to_all(fourier, 'ma', split_axis=2, con...  14.5 us
    all_to_all x1, starting transfers between devices, per_device(): lax.all_to_all(fourier, 'ma', split_axis=2, concat_axis=0, tiled=True)  12.9 us
  transfers between devices with their start and end apart: 2, of which 1 were waited for; matrix products, arithmetic and copies ran while one was open for 27% of the time, Pallas kernels for 0%

commit v1 on v0

v1 whole, which is shorter than its diff:
```python
import functools
import math

import jax
import jax.numpy as jnp
from jax import lax
from jax.experimental import pallas as pl
from jax.experimental.pallas import tpu as pltpu
from jax.sharding import PartitionSpec as P

NLON = 2304
LEV = 64
MESH = pl.DeviceIdType.MESH
BF = jnp.bfloat16
F32 = jnp.float32

GROUP = 64
STRIDE = 37
PAIR_DEV = 6
LANES = 128
TDEV = 18
NJ = 6
DEG = 768


def partner(ma, row, k):
    d = lax.rem(ma + lax.rem(k * STRIDE, GROUP), GROUP)
    half = GROUP // 2
    return d, lax.rem(row + ma // half + d // half, 2)


def kernel(
    spec, basis, last, table, cuts, rot_cos, rot_sin, fine_cos, fine_sin, out,
    stage, bas, own, got, lhs, sendbuf, recvbuf, lon, rx, acc, mix, grid,
    spec_sem, bas_sem, pair_send, pair_recv, send_sem, recv_sem, local_sem, out_sem,
):
    ma = lax.axis_index("ma")
    row = lax.axis_index("row")
    side = lax.rem(row + ma // (GROUP // 2), 2)

    def load_spec(p, j):
        return pltpu.make_async_copy(
            spec.at[p, :, :, :, pl.ds(j * LANES, LANES)], stage.at[p, j], spec_sem.at[p, j]
        )

    def load_basis(p):
        return pltpu.make_async_copy(basis.at[p], bas.at[p], bas_sem.at[p])

    for p in range(PAIR_DEV):
        for j in range(NJ):
            load_spec(p, j).start()
    for p in range(PAIR_DEV):
        load_basis(p).start()

    barrier = pltpu.get_barrier_semaphore()
    pl.semaphore_signal(barrier, inc=1, device_id=(ma, 1 - row), device_id_type=MESH)

    def greet(k, carry):
        pl.semaphore_signal(barrier, inc=1, device_id=partner(ma, row, k), device_id_type=MESH)
        return carry

    lax.fori_loop(1, GROUP, greet, 0)

    def pair_copy(p):
        return pltpu.make_async_remote_copy(
            src_ref=own.at[p],
            dst_ref=got.at[p],
            send_sem=pair_send.at[p],
            recv_sem=pair_recv.at[p],
            device_id=(ma, 1 - row),
            device_id_type=MESH,
        )

    def radial(p):
        for j in range(NJ):
            load_spec(p, j).wait()
            for c in range(2):
                modes = stage[p, j, c].reshape(2 * 192, LANES)
                part = jnp.dot(table[...], modes, preferred_element_type=F32).astype(BF)
                own[p, pl.ds(128 * j + 32 * c, 32)] = part[:64].reshape(32, 2, LANES)
                own[p, pl.ds(128 * j + 64 + 32 * c, 32)] = part[64:].reshape(32, 2, LANES)
        own[p, 768] = last[p]

    radial(0)
    pl.semaphore_wait(barrier, GROUP)
    pair_copy(0).start()

    def more(p, carry):
        radial(p)
        pair_copy(p).start()
        return carry

    lax.fori_loop(1, PAIR_DEV, more, 0)

    def clear(i, carry):
        acc[pl.ds(i * 64, 64), :] = jnp.zeros((64, NLON), F32)
        return carry

    lax.fori_loop(0, TDEV, clear, 0)

    def longitude(q):
        cos_b, sin_b = fine_cos[q], fine_sin[q]
        rc, rs = rot_cos[q], rot_sin[q]
        for i in range(NLON // LANES):
            cos_a, sin_a = rc[:, i : i + 1], rs[:, i : i + 1]
            cols = pl.ds(i * LANES, LANES)
            lon[pl.ds(0, 128), cols] = (cos_a * cos_b - sin_a * sin_b).astype(BF)
            lon[pl.ds(128, 128), cols] = (-(sin_a * cos_b + cos_a * sin_b)).astype(BF)

    def latitude(q):
        pair_copy(q).wait_recv()
        cut = cuts[q]
        for j in range(NJ):
            rows = pl.ds(128 * j, 128)
            levels = (
                own[q, rows].reshape(256, LANES).astype(F32)
                + got[q, rows].reshape(256, LANES).astype(F32)
            ).astype(BF).astype(F32)
            low = lax.broadcasted_iota(jnp.int32, (256, LANES), 1) + 128 * j < cut
            below = jnp.where(low, levels, 0.0).astype(BF)
            above = jnp.where(low, 0.0, levels).astype(BF)
            for half in range(2):
                lhs[half, pl.ds(0, 128), pl.ds(128 * j, 128)] = below[128 * half : 128 * half + 128]
                lhs[half, pl.ds(128, 128), pl.ds(128 * j, 128)] = above[128 * half : 128 * half + 128]
        tail = (own[q, 768].astype(F32) + got[q, 768].astype(F32)).astype(BF).astype(F32)
        load_basis(q).wait()
        first = lax.broadcasted_iota(jnp.int32, (1, LANES), 1) * 0 + side == 0
        tails = (
            jnp.where(first, tail[0:1], tail[1:2]),
            jnp.where(first, tail[1:2], tail[0:1]),
        )

        def block(t0, which, lo, hi):
            half = side if which == 0 else 1 - side
            cols = pl.ds(t0, 128)
            got_t = lax.dot_general(
                bas[q, pl.ds(0, DEG), cols],
                lhs[half],
                (((0,), (1,)), ((), ())),
                preferred_element_type=F32,
            )
            edge = jnp.transpose(bas[q, pl.ds(DEG, 1), cols].astype(F32), (1, 0))
            mix[pl.ds(0, 128, 2), :] = got_t[:, :128]
            mix[pl.ds(1, 128, 2), :] = got_t[:, 128:] + edge * tails[which]
            sendbuf[q, pl.ds(t0 + lo, hi - lo)] = (
                mix[pl.ds(2 * lo, 2 * (hi - lo)), :].astype(BF).reshape(hi - lo, 2, LANES)
            )

        for b in range(4):
            block(128 * b, 0, 0, 128)
        block(512, 0, 0, 64)
        block(512, 1, 64, 128)
        for b in range(5, 9):
            block(128 * b, 1, 0, 128)

    def scatter_copy(q, k):
        d, r = partner(ma, row, k)
        return pltpu.make_async_remote_copy(
            src_ref=sendbuf.at[q, pl.ds(TDEV * d, TDEV)],
            dst_ref=recvbuf.at[q, :, ma],
            send_sem=send_sem.at[q],
            recv_sem=recv_sem.at[q],
            device_id=(d, r),
            device_id_type=MESH,
        )

    def scatter(q):
        def send(k, carry):
            scatter_copy(q, k).start()
            return carry

        lax.fori_loop(1, GROUP, send, 0)
        pltpu.make_async_copy(
            sendbuf.at[q, pl.ds(TDEV * ma, TDEV)], recvbuf.at[q, :, ma], local_sem.at[q]
        ).start()

    def arrive(q):
        pltpu.make_async_copy(
            sendbuf.at[q, pl.ds(TDEV * ma, TDEV)], recvbuf.at[q, :, ma], local_sem.at[q]
        ).wait()
        pltpu.make_async_copy(
            recvbuf.at[q, :, pl.ds(0, GROUP - 1)],
            recvbuf.at[q, :, pl.ds(0, GROUP - 1)],
            recv_sem.at[q],
        ).wait()
        for t in range(TDEV):
            turned = recvbuf[q, t].reshape(128, LANES).T
            rx[pl.ds(64 * t, 64), pl.ds(0, 128)] = turned[:64]
            rx[pl.ds(64 * t, 64), pl.ds(128, 128)] = turned[64:]

    def receive(q):
        longitude(q)
        arrive(q)
        for g in range(3):
            rows = pl.ds(384 * g, 384)
            left = rx[rows, :]
            for n in range(9):
                cols = pl.ds(256 * n, 256)
                acc[rows, cols] += jnp.dot(left, lon[:, cols], preferred_element_type=F32)

    latitude(0)
    scatter(0)

    def step(q, carry):
        latitude(q)
        scatter(q)
        receive(q - 1)
        return carry

    lax.fori_loop(1, PAIR_DEV, step, 0)

    end = PAIR_DEV - 1
    longitude(end)
    arrive(end)

    def put(t, n):
        return pltpu.make_async_copy(
            grid.at[t, n], out.at[:, t, :, pl.ds(n * LANES, LANES)], out_sem
        )

    for g in range(9):
        rows = pl.ds(128 * g, 128)
        left = rx[rows, :]
        for n in range(9):
            cols = pl.ds(256 * n, 256)
            total = (
                acc[rows, cols] + jnp.dot(left, lon[:, cols], preferred_element_type=F32)
            ).astype(BF)
            for a in range(2):
                for b in range(2):
                    grid[2 * g + a, 2 * n + b] = total[
                        64 * a : 64 * a + 64, 128 * b : 128 * b + 128
                    ].reshape(32, 2, LANES)
        for a in range(2):
            for n in range(18):
                put(2 * g + a, n).start()

    def drain(q, carry):
        pair_copy(q).wait_send()
        pltpu.make_async_copy(
            sendbuf.at[q, pl.ds(0, TDEV * (GROUP - 1))],
            sendbuf.at[q, pl.ds(0, TDEV * (GROUP - 1))],
            send_sem.at[q],
        ).wait()
        return carry

    lax.fori_loop(0, PAIR_DEV, drain, 0)
    pltpu.make_async_copy(grid, grid, out_sem).wait()


def radial_table(total_modes, levels):
    mode_index = lax.broadcasted_iota(jnp.int32, (total_modes, levels), 0)
    points = lax.broadcasted_iota(jnp.int32, (total_modes, levels), 1)
    period = 2 * (total_modes - 1)
    phase_steps = mode_index * points % period
    return jnp.cos(phase_steps.astype(F32) * (2.0 * math.pi / period)).astype(BF)


def angles_of(orders, steps):
    return (orders * steps % NLON).astype(F32) * (2.0 * math.pi / NLON)


def per_device(spectral, latitude_basis, pair_orders):
    pair_dev, parts, local_modes, fields, packed = spectral.shape
    degrees = packed - 1
    row_count = lax.axis_size("row")
    level_dev = LEV // row_count
    cheb = lax.dynamic_slice_in_dim(
        radial_table(local_modes * row_count, LEV), lax.axis_index("row") * local_modes, local_modes, 0
    )
    eye = jnp.eye(fields, dtype=BF)
    table = (cheb.T[:, None, :, None] * eye[None, :, None, :]).reshape(
        LEV * fields, local_modes * fields
    )
    last = jnp.einsum(
        "pckf,kl->pclf", spectral[..., degrees], cheb, preferred_element_type=F32
    ).astype(BF)
    last = last.reshape(pair_dev, parts, row_count, level_dev * fields)
    last = jnp.transpose(last, (0, 2, 1, 3)).reshape(pair_dev, row_count, LANES)
    local_orders = lax.dynamic_slice_in_dim(
        pair_orders, lax.axis_index("ma") * pair_dev, pair_dev, 0
    )
    cuts = degrees - local_orders
    orders = jnp.stack([pair_orders, degrees - 1 - pair_orders], axis=1)
    orders = jnp.transpose(orders.reshape(GROUP, pair_dev, 2), (1, 0, 2)).reshape(
        pair_dev, GROUP * 2, 1
    )
    lanes = lax.broadcasted_iota(jnp.int32, (1, 1, LANES), 2)
    weights = jnp.where(orders == 0, 1.0, 2.0).astype(F32)
    coarse = angles_of(orders, lanes[..., : NLON // LANES] * LANES)
    fine = angles_of(orders, lanes)
    result = pl.pallas_call(
        kernel,
        out_shape=jax.ShapeDtypeStruct((level_dev, TDEV, fields, NLON), BF),
        in_specs=[
            pl.BlockSpec(memory_space=pl.ANY),
            pl.BlockSpec(memory_space=pl.ANY),
            pl.BlockSpec(memory_space=pltpu.VMEM),
            pl.BlockSpec(memory_space=pltpu.VMEM),
            pl.BlockSpec(memory_space=pltpu.SMEM),
        ]
        + [pl.BlockSpec(memory_space=pltpu.VMEM)] * 4,
        out_specs=pl.BlockSpec(memory_space=pl.ANY),
        scratch_shapes=[
            pltpu.VMEM((pair_dev, NJ, parts, local_modes, fields, LANES), BF),
            pltpu.VMEM((pair_dev, packed, 1152), BF),
            pltpu.VMEM((pair_dev, packed, 2, LANES), BF),
            pltpu.VMEM((pair_dev, packed, 2, LANES), BF),
            pltpu.VMEM((2, 256, degrees), BF),
            pltpu.VMEM((pair_dev, 1152, 2, LANES), BF),
            pltpu.VMEM((pair_dev, TDEV, GROUP, 2, LANES), BF),
            pltpu.VMEM((256, NLON), BF),
            pltpu.VMEM((1152, 256), BF),
            pltpu.VMEM((1152, NLON), F32),
            pltpu.VMEM((256, LANES), F32),
            pltpu.VMEM((TDEV, NLON // LANES, level_dev, fields, LANES), BF),
            pltpu.SemaphoreType.DMA((pair_dev, NJ)),
            pltpu.SemaphoreType.DMA((pair_dev,)),
            pltpu.SemaphoreType.DMA((pair_dev,)),
            pltpu.SemaphoreType.DMA((pair_dev,)),
            pltpu.SemaphoreType.DMA((pair_dev,)),
            pltpu.SemaphoreType.DMA((pair_dev,)),
            pltpu.SemaphoreType.DMA((pair_dev,)),
            pltpu.SemaphoreType.DMA,
        ],
        compiler_params=pltpu.CompilerParams(
            collective_id=0, has_side_effects=True, vmem_limit_bytes=66_000_000
        ),
    )(
        spectral,
        latitude_basis,
        last,
        table,
        cuts,
        weights * jnp.cos(coarse),
        weights * jnp.sin(coarse),
        jnp.cos(fine),
        jnp.sin(fine),
    )
    return jnp.transpose(result, (0, 2, 1, 3))


def solution(mesh):
    return jax.shard_map(
        per_device,
        mesh=mesh,
        in_specs=(P("ma", None, "row", None, None), P("ma", None, None), P()),
        out_specs=P("row", None, "ma", None),
        check_vma=False,
    )
```

time: 251 us -> 114 us (0.45)
  local copies, waits for them, and re-layouts: 105 us -> 19.9 us
  Pallas kernels: 0 us -> 81.9 us
  waiting for transfers between devices: 61.1 us -> 0 us
  matrix products: 28.3 us -> 0.12 us
  other arithmetic: 35.3 us -> 11.9 us
  starting transfers between devices: 19.1 us -> 0 us
    pallas_call x0 -> x1, Pallas kernels: none -> 81.9 us  [per_device(): pl.pallas_call(kernel, out_shape=jax.ShapeDtypeStruct((level_dev, TDEV, f...]
    all_to_all x2 -> x0, waiting for transfers between devices: 61.1 us -> none  [the longest x1 61.1 us: sum_at_owner(): lax.all_to_all(tiles, axis, split_axis=0, concat_axis=0, tiled=True)]
    reshape x5 -> x2, local copies, waits for them, and re-layouts: 32.5 us -> 0.74 us  [the longest x1 0.68 us: per_device(): last = jnp.transpose(last, (0, 2, 1, 3)).reshape(pair_dev, row_count, LANES)]
    another operation x3 -> x0, other arithmetic: 31.7 us -> none
    dot_general x3 -> x1, matrix products: 28.3 us -> 0.12 us  [per_device(): jnp.einsum('pckf,kl->pclf', spectral[..., degrees], cheb, preferred_eleme...]
    another operation x3 -> x4, local copies, waits for them, and re-layouts: 21.3 us -> 1.1 us  [per_device(): orders = jnp.stack([pair_orders, degrees - 1 - pair_orders], axis=1)]
    all_to_all x2 -> x0, starting transfers between devices: 19.1 us -> none  [the longest x1 12.9 us: per_device(): lax.all_to_all(fourier, 'ma', split_axis=2, concat_axis=0, tiled=True)]
    convert_element_type x2, local copies, waits for them, and re-layouts: 18.6 us -> 0.34 us  [the longest x1 0.18 us: angles_of(): return (orders * steps % NLON).astype(F32) * (2.0 * math.pi / NLON)]
  transfers between devices with their start and end apart: 2 -> 0, of which waited for: 1 -> 0; matrix products, arithmetic and copies ran while one was open for 27% -> 0% of each run, Pallas kernels for 0% -> 0%
where the time goes in v1:
time: 114 us
  Pallas kernels  81.9 us (72%)
  local copies, waits for them, and re-layouts  19.9 us (17%)
  other arithmetic  11.9 us (10%)
    pallas_call x1, Pallas kernels, per_device(): pl.pallas_call(kernel, out_shape=jax.ShapeDtypeStruct((level_dev, TDEV, f...  81.9 us
    mul x1, local copies, waits for them, and re-layouts, per_device(): cheb.T[:, None, :, None] * eye[None, :, None, :]  10.1 us
    unnamed x2, local copies, waits for them, and re-layouts  7.35 us
    mul x1, other arithmetic, per_device(): cheb.T[:, None, :, None] * eye[None, :, None, :]  4.12 us
    sin x1, other arithmetic, per_device(): jnp.sin(fine)  2.65 us
    mul x1, other arithmetic, per_device(): weights * jnp.sin(coarse)  2.39 us

profile of v1, /device:TPU:1, one launch (start us, length us, event | category | flops | bytes accessed | tf_op | source)
XLA Modules:
  0.0 114.0 jit_solution(12655942912166197702)
XLA Ops:
  0.0 0.0 slice-start
  0.0 1.4 %dynamic-slice_subtract_fusion.cuts = s32[6]{0:T(128)} fusion(s32[384]{0:T(512)} %param.5, s32[]{:T(128)S(6)} %select_n.36), kind=kLoop, calls=%fused_computation.36 | loop fusion | flops 6 | bytes 52 | tf_op jit(solution)/shard_map/sub | solution.py:283
  1.4 0.7 broadcast_subtract_fusion
  2.1 0.1 stack.10
  2.3 0.1 copy.25
  2.3 0.8 stack.9
  3.2 0.1 copy.24
  3.3 0.1 fusion.8
  3.3 0.1 copy.26
  3.5 0.1 copy.28
  3.5 0.1 copy.27
  3.6 0.1 fusion.10
  3.8 0.3 fusion.17
  4.2 0.2 copy.29
  4.3 2.4 %sine_multiply_fusion = (f32[6,128,18]{2,1,0:T(8,128)}, f32[6,128,18]{2,1,0:T(8,128)}) fusion(f32[6,128,18]{2,1,0:T(8,128)S(1)} %copy.29, f32[6,128]{1,0:T(8,128)S(1)} %copy.27), kind=kLoop, calls=%fused_computation.11 | loop fusion | flops 41472 | bytes 168960 | tf_op jit(solution)/shard_map/mul | solution.py:336
  6.7 2.6 %fusion.5 = (f32[6,128,128]{2,1,0:T(8,128)}, f32[6,128,128]{2,1,0:T(8,128)}) fusion(s32[6,128]{1,0:T(8,128)S(1)} %copy.28), kind=kLoop, calls=%fused_computation.9 | loop fusion | flops 884736 | bytes 789504 | tf_op jit(solution)/shard_map/sin | solution.py:338
  9.4 0.0 slice-done
  9.4 1.3 %copy.32 = bf16[6,2,192,2,1]{2,0,3,1,4:T(8,128)(2,1)S(1)} copy(bf16[6,2,192,2,1]{4,3,2,1,0:T(2,128)(2,1)S(1)} %slice-done) | data formatting | bytes 18432
  10.6 0.1 fusion
  10.8 0.2 copy.22
  10.9 0.1 copy.23
  11.0 0.7 reshape.38.last
  11.7 4.1 %broadcast_multiply_fusion = bf16[64,2,192,2]{3,2,1,0:T(8,128)(2,1)} fusion(bf16[2,2]{1,0:T(2,128)(2,1)S(1)} %compare_convert_fusion, bf16[64,192]{1,0:T(8,128)(2,1)S(1)} %bitcast.25), kind=kLoop, calls=%fused_computation | loop fusion | flops 49152 | bytes 122888 | tf_op jit(solution)/shard_map/mul | solution.py:272
  15.8 10.1 %mul.96.table = bf16[128,384]{1,0:T(8,128)(2,1)} reshape(bf16[64,2,192,2]{3,2,1,0:T(8,128)(2,1)} %broadcast_multiply_fusion) | data formatting | bytes 196608 | tf_op jit(solution)/shard_map/mul | solution.py:272
  25.9 81.9 %shard_map.37 = bf16[32,18,2,2304]{3,2,1,0:T(2,128)(2,1)} custom-call(bf16[6,2,192,2,769]{4,3,2,1,0:T(2,128)(2,1)} %spec.1, bf16[6,769,1152]{2,1,0:T(8,128)(2,1)} %basis.1, bf16[6,2,128]{2,1,0:T(2,128)(2,1)} %reshape.38.last, bf16[128,384]{1,0:T(8,128)(2,1)} %mul.96.table, s32[6]{0:T(128)} %dynamic-slice_subtract_fusion.cuts, ...), custom_call_target="tpu_custom_call" | custom-call | tf_op jit(solution)/shard_map/pallas_call | solution.py:292
  107.9 6.1 %copy.34 = bf16[32,2,18,2304]{3,1,2,0:T(2,128)(2,1)} copy(bf16[32,2,18,2304]{3,1,2,0:T(2,128)(2,1)} %bitcast.22) | data formatting | bytes 10616832
  (6 shorter events, 0.1 us)
Async XLA Ops:
  0.0 9.4 %slice-start = ((bf16[6,2,192,2,769]{4,3,2,1,0:T(2,128)(2,1)}), bf16[6,2,192,2,1]{4,3,2,1,0:T(2,128)(2,1)S(1)}, s32[]{:S(2)}) async-start(bf16[6,2,192,2,769]{4,3,2,1,0:T(2,128)(2,1)} %spec.1), calls=%async_computation | async-start | bytes 2359296 | tf_op jit(solution)/shard_map/slice | solution.py:276

commit v2 on v0

v2 whole, which is shorter than its diff:
```python
import functools
import math

import jax
import jax.numpy as jnp
from jax import lax
from jax.experimental import pallas as pl
from jax.experimental.pallas import tpu as pltpu
from jax.sharding import PartitionSpec as P

NLON = 2304
LEV = 64
MESH = pl.DeviceIdType.MESH
BF = jnp.bfloat16
F32 = jnp.float32

PLANE = 32
STRIDE = 13
PAIR_DEV = 6
LANES = 128
TDEV = 18
NJ = 6
DEG = 768
MODES = 192
TURN = 2.0 * math.pi


def cosine(steps, period):
    left = steps - period * jnp.floor(steps * (1.0 / period) + 0.5)
    size = jnp.abs(left)
    flip = size > period / 4
    angle = jnp.where(flip, period / 2 - size, size) * (TURN / period)
    square = angle * angle
    total = jnp.full_like(square, -1.0 / math.factorial(14))
    for n in range(12, -1, -2):
        total = total * square + (-1.0) ** (n // 2) / math.factorial(n)
    return jnp.where(flip, -total, total)


def kernel(
    spec, basis, orders_row, orders, out,
    stage, rows, bas, own, got, lhs, sendbuf, recvbuf, lon, rx, acc, mix, table, grid,
    spec_sem, rows_sem, bas_sem, pair_send, pair_recv, send_sem, recv_sem, meet, out_sem,
):
    ma = lax.axis_index("ma")
    row = lax.axis_index("row")
    plane = ma // PLANE
    place = lax.rem(ma, PLANE)
    along_y, along_z, core = place // 8, lax.rem(place // 2, 4), lax.rem(place, 2)

    def load_spec(p, j):
        return pltpu.make_async_copy(
            spec.at[p, :, :, :, pl.ds(j * LANES, LANES)], stage.at[p, j], spec_sem.at[p, j]
        )

    def load_rows(p):
        slot = lax.rem(p, 2)
        return pltpu.make_async_copy(spec.at[p], rows.at[slot], rows_sem.at[slot])

    def load_basis(p):
        return pltpu.make_async_copy(basis.at[p], bas.at[p], bas_sem.at[p])

    for p in range(PAIR_DEV):
        for j in range(NJ):
            load_spec(p, j).start()
        if p < 2:
            load_rows(p).start()
        else:
            load_basis(p - 2).start()
    for p in range(PAIR_DEV - 2, PAIR_DEV):
        load_basis(p).start()

    def signal(sem, device):
        pl.semaphore_signal(sem, inc=1, device_id=device, device_id_type=MESH)

    def on_y(i):
        return plane * PLANE + lax.rem(along_y + i, 4) * 8 + along_z * 2 + core, row

    def on_z(i):
        return plane * PLANE + along_y * 8 + lax.rem(along_z + i, 4) * 2 + core, row

    across = ((1 - plane) * PLANE + place, 1 - row)
    barrier = pltpu.get_barrier_semaphore()
    signal(barrier, (ma, 1 - row))
    for i in range(1, 4):
        signal(barrier, on_y(i))
    for i in range(1, 4):
        signal(barrier, on_z(i))
    signal(barrier, (plane * PLANE + along_y * 8 + along_z * 2 + 1 - core, row))
    signal(barrier, across)

    level = lax.broadcasted_iota(jnp.int32, (LANES, 2 * MODES), 0)
    mode = lax.broadcasted_iota(jnp.int32, (LANES, 2 * MODES), 1)
    steps = (level // 2) * (mode // 2 + row * MODES)
    same = lax.rem(level, 2) == lax.rem(mode, 2)
    period = 2 * (2 * MODES - 1)
    table[...] = jnp.where(same, cosine(steps.astype(F32), period), 0.0).astype(BF)

    def pair_copy(p, w):
        half = row if w == 0 else 1 - row
        return pltpu.make_async_remote_copy(
            src_ref=own.at[p, half],
            dst_ref=got.at[p, half],
            send_sem=pair_send.at[p, w],
            recv_sem=pair_recv.at[p, w],
            device_id=(ma, 1 - row),
            device_id_type=MESH,
        )

    def radial(p):
        ends = []
        for j in range(NJ):
            load_spec(p, j).wait()
            for c in range(2):
                modes = stage[p, j, c].reshape(2 * MODES, LANES)
                part = jnp.dot(table[...], modes, preferred_element_type=F32).astype(BF)
                for half in range(2):
                    own[p, half, pl.ds(64 * j + 32 * c, 32)] = part[
                        64 * half : 64 * half + 64
                    ].reshape(32, 2, LANES)
        load_rows(p).wait()
        for c in range(2):
            modes = rows[lax.rem(p, 2), c, :, :, DEG : DEG + 1].reshape(2 * MODES, 1)
            ends.append(
                lax.dot_general(
                    modes, table[...], (((0,), (1,)), ((), ())), preferred_element_type=F32
                )
            )
        for half in range(2):
            joined = jnp.concatenate([e[:, 64 * half : 64 * half + 64] for e in ends], axis=1)
            own[p, half, 64 * NJ] = jnp.broadcast_to(joined.astype(BF), (2, LANES))

    def more(p):
        radial(p)
        pair_copy(p, 0).start()
        pair_copy(p, 1).start()

    def longitude(q):
        k = lax.broadcasted_iota(jnp.int32, (LANES, PLANE * 2 * PAIR_DEV), 0)
        slot = lax.broadcasted_iota(jnp.int32, (LANES, PLANE * 2 * PAIR_DEV), 1)
        picked = jnp.where(slot == (k // 2) * PAIR_DEV + q, orders_row[...].reshape(1, PLANE * 2 * PAIR_DEV).astype(F32), 0.0)
        lower = jnp.sum(picked, axis=1, keepdims=True)
        odd = lax.rem(lax.broadcasted_iota(jnp.int32, (LANES, 1), 0), 2) == 1
        order = jnp.where(odd, DEG - 1 - lower, lower)
        weight = jnp.where(order == 0, 1.0, 2.0)
        lane = lax.broadcasted_iota(jnp.int32, (LANES, LANES), 1).astype(F32)
        fine = order * lane
        cos_b, sin_b = cosine(fine, NLON), cosine(fine - NLON // 4, NLON)
        coarse = order * jnp.where(lane < NLON // LANES, lane, 0.0) * LANES
        cos_all = weight * cosine(coarse, NLON)
        sin_all = weight * cosine(coarse - NLON // 4, NLON)
        for i in range(NLON // LANES):
            cos_a, sin_a = cos_all[:, i : i + 1], sin_all[:, i : i + 1]
            cols = pl.ds(i * LANES, LANES)
            lon[pl.ds(0, 128), cols] = (cos_a * cos_b - sin_a * sin_b).astype(BF)
            lon[pl.ds(128, 128), cols] = (-(sin_a * cos_b + cos_a * sin_b)).astype(BF)

    def latitude(q, w):
        half = 1 - row if w == 0 else row
        to = 1 - plane if w == 0 else plane
        pair_copy(q, w).wait_recv()
        cut = DEG - orders[ma * PAIR_DEV + q]
        for j in range(NJ):
            piece = pl.ds(64 * j, 64)
            levels = (
                own[q, half, piece].reshape(128, LANES).astype(F32)
                + got[q, half, piece].reshape(128, LANES).astype(F32)
            )
            low = lax.broadcasted_iota(jnp.int32, (128, LANES), 1) + 128 * j < cut
            lhs[w, pl.ds(0, 128), pl.ds(128 * j, 128)] = jnp.where(low, levels, 0.0).astype(BF)
            lhs[w, pl.ds(128, 128), pl.ds(128 * j, 128)] = jnp.where(low, 0.0, levels).astype(BF)
        end = own[q, half, 64 * NJ].astype(F32) + got[q, half, 64 * NJ].astype(F32)
        end = end.astype(BF).astype(F32)[0:1]
        if w == 0:
            load_basis(q).wait()
        for b in range(5):
            cols = pl.ds(pl.multiple_of(to * 512 + 128 * b, 128), 128)
            made = lax.dot_general(
                bas[q, pl.ds(0, DEG), cols],
                lhs[w],
                (((0,), (1,)), ((), ())),
                preferred_element_type=F32,
            )
            edge = jnp.transpose(bas[q, pl.ds(DEG, 1), cols].astype(F32), (1, 0))
            mix[b % 2, pl.ds(0, 128, 2), :] = made[:, :128]
            mix[b % 2, pl.ds(1, 128, 2), :] = made[:, 128:] + edge * end
            sendbuf[q, w, pl.ds(128 * b, 128)] = mix[b % 2].astype(BF).reshape(128, 2, LANES)

    def scatter_copy(q, w, k):
        to = 1 - plane if w == 0 else plane
        other = lax.rem(place + lax.rem(k * STRIDE, PLANE), PLANE)
        return pltpu.make_async_remote_copy(
            src_ref=sendbuf.at[q, w, pl.ds(64 * to + TDEV * other, TDEV)],
            dst_ref=recvbuf.at[q, :, ma],
            send_sem=send_sem.at[q, w],
            recv_sem=recv_sem.at[q, w],
            device_id=(to * PLANE + other, 1 - row if w == 0 else row),
            device_id_type=MESH,
        )

    def scatter_across(q):
        def send(k, carry):
            scatter_copy(q, 0, k).start()
            return carry

        lax.fori_loop(0, PLANE, send, 0, unroll=4)

    def keep(q):
        return pltpu.make_async_copy(
            sendbuf.at[q, 1, pl.ds(64 * plane + TDEV * place, TDEV)],
            recvbuf.at[q, :, ma],
            recv_sem.at[q, 1],
        )

    def scatter_inside(q):
        def send(k, carry):
            scatter_copy(q, 1, k).start()
            return carry

        lax.fori_loop(1, PLANE, send, 0, unroll=4)
        keep(q).start()

    def scatter_both(q):
        scatter_copy(q, 0, 0).start()

        def send(k, carry):
            scatter_copy(q - 1, 1, k).start()
            scatter_copy(q, 0, k).start()
            return carry

        lax.fori_loop(1, PLANE, send, 0, unroll=2)
        keep(q - 1).start()

    def arrive(q):
        for w in range(2):
            arrived = recvbuf.at[q, :, pl.ds((1 - plane if w == 0 else plane) * PLANE, PLANE)]
            pltpu.make_async_copy(arrived, arrived, recv_sem.at[q, w]).wait()
        for t in range(TDEV):
            turned = recvbuf[q, t].reshape(128, LANES).T
            rx[pl.ds(64 * t, 64), pl.ds(0, 128)] = turned[:64]
            rx[pl.ds(64 * t, 64), pl.ds(128, 128)] = turned[64:]

    def receive(q, first=False):
        arrive(q)
        for g in range(3):
            part = pl.ds(384 * g, 384)
            left = rx[part, :]
            for n in range(9):
                cols = pl.ds(256 * n, 256)
                added = jnp.dot(left, lon[:, cols], preferred_element_type=F32)
                acc[part, cols] = added if first else acc[part, cols] + added

    radial(0)
    pl.semaphore_wait(barrier, 9)
    pair_copy(0, 0).start()
    pair_copy(0, 1).start()
    load_rows(2).start()
    for i in range(1, 4):
        signal(meet.at[0], on_y(i))
    more(1)
    load_rows(3).start()
    pl.semaphore_wait(meet.at[0], 3)
    for i in range(1, 4):
        signal(meet.at[1], on_z(i))
    longitude(0)
    pl.semaphore_wait(meet.at[1], 3)
    signal(meet.at[2], across)
    latitude(0, 0)
    pl.semaphore_wait(meet.at[2], 1)
    scatter_across(0)
    more(2)
    load_rows(4).start()
    latitude(0, 1)
    latitude(1, 0)
    scatter_both(1)
    more(3)
    load_rows(5).start()
    latitude(1, 1)
    latitude(2, 0)
    scatter_both(2)
    more(4)
    receive(0, True)
    longitude(1)
    latitude(2, 1)

    def step(q, carry):
        latitude(q, 0)
        scatter_both(q)

        @pl.when(q < PAIR_DEV - 2)
        def _():
            more(q + 2)

        receive(q - 2)
        longitude(q - 1)
        latitude(q, 1)
        return carry

    lax.fori_loop(3, PAIR_DEV, step, 0)

    end = PAIR_DEV - 1
    scatter_inside(end)
    receive(end - 1)
    longitude(end)
    arrive(end)

    def put(t):
        return pltpu.make_async_copy(grid.at[t], out.at[:, t], out_sem.at[t])

    for g in range(9):
        part = pl.ds(128 * g, 128)
        left = rx[part, :]
        for n in range(9):
            cols = pl.ds(256 * n, 256)
            total = (
                acc[part, cols] + jnp.dot(left, lon[:, cols], preferred_element_type=F32)
            ).astype(BF)
            for a in range(2):
                for b in range(2):
                    grid[2 * g + a, :, :, pl.ds(256 * n + 128 * b, LANES)] = total[
                        64 * a : 64 * a + 64, 128 * b : 128 * b + 128
                    ].reshape(32, 2, LANES)
        for a in range(2):
            put(2 * g + a).start()

    def drain(q, carry):
        for w in range(2):
            pair_copy(q, w).wait_send()
            sent = sendbuf.at[q, w, pl.ds(0, TDEV * (PLANE - w))]
            pltpu.make_async_copy(sent, sent, send_sem.at[q, w]).wait()
        return carry

    lax.fori_loop(0, PAIR_DEV, drain, 0)
    for t in range(TDEV):
        put(t).wait()


def write_out(grid, out, hold, read_sem, write_sem):
    reads, writes = [], []
    for i in range(8):
        piece = pl.ds(4 * i, 4)
        reads.append(pltpu.make_async_copy(grid.at[piece], hold.at[i], read_sem.at[i]))
        writes.append(pltpu.make_async_copy(hold.at[i], out.at[piece], write_sem.at[i]))
    for copy in reads:
        copy.start()
    for read, write in zip(reads, writes):
        read.wait()
        write.start()
    for copy in writes:
        copy.wait()


def per_device(spectral, latitude_basis, pair_orders):
    pair_dev, parts, local_modes, fields, packed = spectral.shape
    degrees = packed - 1
    level_dev = LEV // lax.axis_size("row")
    shape = jax.ShapeDtypeStruct((level_dev, TDEV, fields, NLON), BF)
    grid = pl.pallas_call(
        kernel,
        out_shape=shape,
        in_specs=[
            pl.BlockSpec(memory_space=pl.ANY),
            pl.BlockSpec(memory_space=pl.ANY),
            pl.BlockSpec(memory_space=pltpu.VMEM),
            pl.BlockSpec(memory_space=pltpu.SMEM),
        ],
        out_specs=pl.BlockSpec(memory_space=pl.ANY),
        scratch_shapes=[
            pltpu.VMEM((pair_dev, NJ, parts, local_modes, fields, LANES), BF),
            pltpu.VMEM((2, parts, local_modes, fields, packed), BF),
            pltpu.VMEM((pair_dev, packed, 1152), BF),
            pltpu.VMEM((pair_dev, 2, 64 * NJ + 1, 2, LANES), BF),
            pltpu.VMEM((pair_dev, 2, 64 * NJ + 1, 2, LANES), BF),
            pltpu.VMEM((2, 256, degrees), BF),
            pltpu.VMEM((pair_dev, 2, 640, 2, LANES), BF),
            pltpu.VMEM((pair_dev, TDEV, 2 * PLANE, 2, LANES), BF),
            pltpu.VMEM((256, NLON), BF),
            pltpu.VMEM((1152, 256), BF),
            pltpu.VMEM((1152, NLON), F32),
            pltpu.VMEM((2, 256, LANES), F32),
            pltpu.VMEM((LANES, fields * local_modes), BF),
            pltpu.VMEM((TDEV, level_dev, fields, NLON), BF),
            pltpu.SemaphoreType.DMA((pair_dev, NJ)),
            pltpu.SemaphoreType.DMA((2,)),
            pltpu.SemaphoreType.DMA((pair_dev,)),
            pltpu.SemaphoreType.DMA((pair_dev, 2)),
            pltpu.SemaphoreType.DMA((pair_dev, 2)),
            pltpu.SemaphoreType.DMA((pair_dev, 2)),
            pltpu.SemaphoreType.DMA((pair_dev, 2)),
            pltpu.SemaphoreType.REGULAR((3,)),
            pltpu.SemaphoreType.DMA((TDEV,)),
        ],
        compiler_params=pltpu.CompilerParams(
            collective_id=0, has_side_effects=True, vmem_limit_bytes=60 * 2**20
        ),
    )(spectral, latitude_basis, pair_orders, pair_orders)
    result = pl.pallas_call(
        write_out,
        out_shape=shape,
        in_specs=[pl.BlockSpec(memory_space=pl.ANY)],
        out_specs=pl.BlockSpec(memory_space=pl.ANY),
        scratch_shapes=[
            pltpu.VMEM((8, level_dev // 8, TDEV, fields, NLON), BF),
            pltpu.SemaphoreType.DMA((8,)),
            pltpu.SemaphoreType.DMA((8,)),
        ],
        compiler_params=pltpu.CompilerParams(vmem_limit_bytes=63 * 2**20),
    )(grid)
    return jnp.transpose(result, (0, 2, 1, 3))


def solution(mesh):
    return jax.shard_map(
        per_device,
        mesh=mesh,
        in_specs=(P("ma", None, "row", None, None), P("ma", None, None), P()),
        out_specs=P("row", None, "ma", None),
        check_vma=False,
    )
```

time: 251 us -> 86.1 us (0.34)
  local copies, waits for them, and re-layouts: 105 us -> 0 us
  Pallas kernels: 0 us -> 85.7 us
  waiting for transfers between devices: 61.1 us -> 0 us
  other arithmetic: 35.3 us -> 0 us
  matrix products: 28.3 us -> 0 us
  starting transfers between devices: 19.1 us -> 0 us
    pallas_call x0 -> x2, Pallas kernels: none -> 85.7 us  [the longest x1 81 us: per_device(): pl.pallas_call(kernel, out_shape=shape, in_specs=[pl.BlockSpec(memory_spa...]
    all_to_all x2 -> x0, waiting for transfers between devices: 61.1 us -> none  [the longest x1 61.1 us: sum_at_owner(): lax.all_to_all(tiles, axis, split_axis=0, concat_axis=0, tiled=True)]
    reshape x5 -> x0, local copies, waits for them, and re-layouts: 32.5 us -> none  [the longest x2 17.3 us: per_device(): synthesized.reshape(level_dev, fields, synthesized.shape[1], synthesized....]
    another operation x3 -> x0, other arithmetic: 31.7 us -> none
    dot_general x3 -> x0, matrix products: 28.3 us -> none  [the longest x1 14.5 us: per_device(): jnp.einsum('oit,on->itn', lax.all_to_all(fourier, 'ma', split_axis=2, con...]
    unnamed x8 -> x0, local copies, waits for them, and re-layouts: 24.7 us -> none
    another operation x3 -> x0, local copies, waits for them, and re-layouts: 21.3 us -> none  [the longest x1 21.3 us: longitude_table(): stacked = jnp.stack([real_part, imag_part], axis=2)]
    all_to_all x2 -> x0, starting transfers between devices: 19.1 us -> none  [the longest x1 12.9 us: per_device(): lax.all_to_all(fourier, 'ma', split_axis=2, concat_axis=0, tiled=True)]
  transfers between devices with their start and end apart: 2 -> 0, of which waited for: 1 -> 0; matrix products, arithmetic and copies ran while one was open for 27% -> 0% of each run, Pallas kernels for 0% -> 0%
where the time goes in v2:
time: 86.1 us; the launch traced here: 85.9 us
  Pallas kernels  85.7 us (100%)
    pallas_call x1, Pallas kernels, per_device(): pl.pallas_call(kernel, out_shape=shape, in_specs=[pl.BlockSpec(memory_spa...  81 us
    pallas_call x1, Pallas kernels, per_device(): pl.pallas_call(write_out, out_shape=shape, in_specs=[pl.BlockSpec(memory_...  4.68 us

profile of v2, /device:TPU:1, one launch (start us, length us, event | category | flops | bytes accessed | tf_op | source)
XLA Modules:
  0.0 85.9 jit_solution(6535082975037045004)
XLA Ops:
  0.0 81.0 %shard_map.37.grid = bf16[32,18,2,2304]{3,2,1,0:T(2,128)(2,1)} custom-call(bf16[6,2,192,2,769]{4,3,2,1,0:T(2,128)(2,1)} %spec.1, bf16[6,769,1152]{2,1,0:T(8,128)(2,1)} %basis.1, s32[384]{0:T(512)} %orders.1, s32[384]{0:T(512)} %orders.1), custom_call_target="tpu_custom_call" | custom-call | tf_op jit(solution)/shard_map/pallas_call | solution.py:358
  81.0 4.7 %shard_map.38 = bf16[32,18,2,2304]{3,2,1,0:T(2,128)(2,1)} custom-call(bf16[32,18,2,2304]{3,2,1,0:T(2,128)(2,1)} %shard_map.37.grid), custom_call_target="tpu_custom_call" | custom-call | tf_op jit(solution)/shard_map/pallas_call | solution.py:397

commit v3 on v2

--- a/solution.py
+++ b/solution.py
@@ -15,7 +15,7 @@
 F32 = jnp.float32
 
 PLANE = 32
-STRIDE = 13
+STRIDE = 5
 PAIR_DEV = 6
 LANES = 128
 TDEV = 18
@@ -60,15 +60,20 @@
     def load_basis(p):
         return pltpu.make_async_copy(basis.at[p], bas.at[p], bas_sem.at[p])
 
-    for p in range(PAIR_DEV):
-        for j in range(NJ):
-            load_spec(p, j).start()
-        if p < 2:
-            load_rows(p).start()
-        else:
-            load_basis(p - 2).start()
-    for p in range(PAIR_DEV - 2, PAIR_DEV):
-        load_basis(p).start()
+    for j in range(NJ):
+        load_spec(0, j).start()
+    load_rows(0).start()
+
+    def load_others():
+        for p in range(1, PAIR_DEV):
+            for j in range(NJ):
+                load_spec(p, j).start()
+            if p == 1:
+                load_rows(1).start()
+            else:
+                load_basis(p - 2).start()
+        for p in range(PAIR_DEV - 2, PAIR_DEV):
+            load_basis(p).start()
 
     def signal(sem, device):
         pl.semaphore_signal(sem, inc=1, device_id=device, device_id_type=MESH)
@@ -107,10 +112,12 @@
             device_id_type=MESH,
         )
 
-    def radial(p):
+    def radial(p, first=False):
         ends = []
         for j in range(NJ):
             load_spec(p, j).wait()
+            if first and j == NJ - 1:
+                load_others()
             for c in range(2):
                 modes = stage[p, j, c].reshape(2 * MODES, LANES)
                 part = jnp.dot(table[...], modes, preferred_element_type=F32).astype(BF)
@@ -250,7 +257,7 @@
                 added = jnp.dot(left, lon[:, cols], preferred_element_type=F32)
                 acc[part, cols] = added if first else acc[part, cols] + added
 
-    radial(0)
+    radial(0, True)
     pl.semaphore_wait(barrier, 9)
     pair_copy(0, 0).start()
     pair_copy(0, 1).start()
@@ -262,23 +269,24 @@
     pl.semaphore_wait(meet.at[0], 3)
     for i in range(1, 4):
         signal(meet.at[1], on_z(i))
-    longitude(0)
+    more(2)
+    load_rows(4).start()
     pl.semaphore_wait(meet.at[1], 3)
     signal(meet.at[2], across)
+    longitude(0)
+    more(3)
+    load_rows(5).start()
+    pl.semaphore_wait(meet.at[2], 1)
     latitude(0, 0)
-    pl.semaphore_wait(meet.at[2], 1)
     scatter_across(0)
-    more(2)
-    load_rows(4).start()
+    more(4)
     latitude(0, 1)
     latitude(1, 0)
     scatter_both(1)
-    more(3)
-    load_rows(5).start()
+    more(5)
     latitude(1, 1)
     latitude(2, 0)
     scatter_both(2)
-    more(4)
     receive(0, True)
     longitude(1)
     latitude(2, 1)
@@ -286,10 +294,6 @@
     def step(q, carry):
         latitude(q, 0)
         scatter_both(q)
-
-        @pl.when(q < PAIR_DEV - 2)
-        def _():
-            more(q + 2)
 
         receive(q - 2)
         longitude(q - 1)

time: 86.1 us -> 82.1 us (0.954)
  Pallas kernels: 85.7 us -> 81.8 us
    pallas_call x1, Pallas kernels: 81 us -> 77.1 us  [per_device(): pl.pallas_call(kernel, out_shape=shape, in_specs=[pl.BlockSpec(memory_spa...]
where the time goes in v3:
time: 82.1 us; the launch traced here: 81.9 us
  Pallas kernels  81.8 us (100%)
    pallas_call x1, Pallas kernels, per_device(): pl.pallas_call(kernel, out_shape=shape, in_specs=[pl.BlockSpec(memory_spa...  77.1 us
    pallas_call x1, Pallas kernels, per_device(): pl.pallas_call(write_out, out_shape=shape, in_specs=[pl.BlockSpec(memory_...  4.68 us

profile of v3, /device:TPU:1, one launch (start us, length us, event | category | flops | bytes accessed | tf_op | source)
XLA Modules:
  0.0 81.9 jit_solution(8459552793330455666)
XLA Ops:
  0.0 77.1 %shard_map.37.grid = bf16[32,18,2,2304]{3,2,1,0:T(2,128)(2,1)} custom-call(bf16[6,2,192,2,769]{4,3,2,1,0:T(2,128)(2,1)} %spec.1, bf16[6,769,1152]{2,1,0:T(8,128)(2,1)} %basis.1, s32[384]{0:T(512)} %orders.1, s32[384]{0:T(512)} %orders.1), custom_call_target="tpu_custom_call" | custom-call | tf_op jit(solution)/shard_map/pallas_call | solution.py:362
  77.1 4.7 %shard_map.38 = bf16[32,18,2,2304]{3,2,1,0:T(2,128)(2,1)} custom-call(bf16[32,18,2,2304]{3,2,1,0:T(2,128)(2,1)} %shard_map.37.grid), custom_call_target="tpu_custom_call" | custom-call | tf_op jit(solution)/shard_map/pallas_call | solution.py:401

commit v4 on v3

--- a/solution.py
+++ b/solution.py
@@ -15,7 +15,7 @@
 F32 = jnp.float32
 
 PLANE = 32
-STRIDE = 5
+STRIDE = 11
 PAIR_DEV = 6
 LANES = 128
 TDEV = 18
@@ -341,8 +341,8 @@
 
 def write_out(grid, out, hold, read_sem, write_sem):
     reads, writes = [], []
-    for i in range(8):
-        piece = pl.ds(4 * i, 4)
+    for i in range(4):
+        piece = pl.ds(8 * i, 8)
         reads.append(pltpu.make_async_copy(grid.at[piece], hold.at[i], read_sem.at[i]))
         writes.append(pltpu.make_async_copy(hold.at[i], out.at[piece], write_sem.at[i]))
     for copy in reads:
@@ -404,9 +404,9 @@
         in_specs=[pl.BlockSpec(memory_space=pl.ANY)],
         out_specs=pl.BlockSpec(memory_space=pl.ANY),
         scratch_shapes=[
-            pltpu.VMEM((8, level_dev // 8, TDEV, fields, NLON), BF),
-            pltpu.SemaphoreType.DMA((8,)),
-            pltpu.SemaphoreType.DMA((8,)),
+            pltpu.VMEM((4, level_dev // 4, TDEV, fields, NLON), BF),
+            pltpu.SemaphoreType.DMA((4,)),
+            pltpu.SemaphoreType.DMA((4,)),
         ],
         compiler_params=pltpu.CompilerParams(vmem_limit_bytes=63 * 2**20),
     )(grid)

time: 82.1 us -> 82.1 us (level)
  no operation moved by 1% of the time
where the time goes in v4:
time: 82.1 us; the launch traced here: 81.8 us
  Pallas kernels  81.6 us (99%)
    pallas_call x1, Pallas kernels, per_device(): pl.pallas_call(kernel, out_shape=shape, in_specs=[pl.BlockSpec(memory_spa...  77.3 us
    pallas_call x1, Pallas kernels, per_device(): pl.pallas_call(write_out, out_shape=shape, in_specs=[pl.BlockSpec(memory_...  4.29 us

profile of v4, /device:TPU:1, one launch (start us, length us, event | category | flops | bytes accessed | tf_op | source)
XLA Modules:
  0.0 81.8 jit_solution(1737960121806898649)
XLA Ops:
  0.0 77.3 %shard_map.37.grid = bf16[32,18,2,2304]{3,2,1,0:T(2,128)(2,1)} custom-call(bf16[6,2,192,2,769]{4,3,2,1,0:T(2,128)(2,1)} %spec.1, bf16[6,769,1152]{2,1,0:T(8,128)(2,1)} %basis.1, s32[384]{0:T(512)} %orders.1, s32[384]{0:T(512)} %orders.1), custom_call_target="tpu_custom_call" | custom-call | tf_op jit(solution)/shard_map/pallas_call | solution.py:362
  77.3 4.3 %shard_map.38 = bf16[32,18,2,2304]{3,2,1,0:T(2,128)(2,1)} custom-call(bf16[32,18,2,2304]{3,2,1,0:T(2,128)(2,1)} %shard_map.37.grid), custom_call_target="tpu_custom_call" | custom-call | tf_op jit(solution)/shard_map/pallas_call | solution.py:401
